TPU v7x, 16 devices: a 4x2x1 block of a 4x4x8 slice. The times are simulated.
16 devices in a mesh: dp: 2 (over y, z), cp: 8 (over x, core).
Axes of the slice: x: 4, y: 2, z: 1, core: 2. Of those that a mesh axis runs over, the one named last changes fastest.
The devices are a block of a 4x4x8 slice.
Arguments:
- x: bfloat16 [4096, 3072], P(('dp', 'cp')), parts along dimension 0
- seg: int32 [4096], P(('dp', 'cp')), parts along dimension 0
- wq: bfloat16 [3072, 3072], replicated
- wk: bfloat16 [3072, 1024], replicated
- wv: bfloat16 [3072, 1024], replicated
- wo: bfloat16 [3072, 3072], replicated
Outputs:
- output: bfloat16 [4096, 3072], P(('dp', 'cp')), parts along dimension 0
There are 2 independent parts. A program takes and returns all parts, laid end to end along the dimension named above; an argument that names none is the same for every part.
All inputs are finite; a program needn't handle non-finite values.
Results may differ from a plain program's by a relative error of at most 0.00626007.
Values are sent between devices in bfloat16 or wider.
A program may use at most 768 MiB of HBM per device.

v0:
```python
import functools
import math

import jax
import jax.numpy as jnp
from jax import lax
from jax.experimental import pallas as pl
from jax.experimental.pallas import tpu as pltpu
from jax.sharding import PartitionSpec as P

DH = 128
F32 = jnp.float32
BF16 = jnp.bfloat16
NEG = float("-inf")
SCALE = math.log2(math.e) * DH ** -0.5


def kernel(
    n, heads, groups,
    x_hbm, seg_hbm, wq_hbm, wk_hbm, wv_hbm, wo_hbm, y_out,
    x_buf, wkv, wq, wo, kv, q_buf, seg_all, bias, s_buf, m_buf, l_buf, c_buf, a_buf, o_buf, o_sib, y_acc,
    x_sem, xs_send, xs_recv, seg_sem, sg_send, sg_recv, wkv_sem, wq_sem, wo_sem,
    own_send, near_recv, fwd_send, far_recv, os_send, os_recv,
):
    chips = n // 2
    piece = x_hbm.shape[1]
    rows = 2 * piece
    dim = x_hbm.shape[2]
    me = lax.axis_index("cp")
    c, h = lax.div(me, 2), lax.rem(me, 2)
    other = 1 - h
    right_chip, left_chip = lax.rem(c + 1, chips), lax.rem(c + chips - 1, chips)
    far_chip = lax.rem(c + chips // 2, chips)
    right, left, sibling = 2 * right_chip + h, 2 * left_chip + h, 2 * c + other
    qcols = heads * groups * DH
    gw = groups * DH
    ph = jax.named_scope

    def remote(src, dst, send, recv, dev):
        return pltpu.make_async_remote_copy(
            src_ref=src, dst_ref=dst, send_sem=send, recv_sem=recv,
            device_id={"cp": dev}, device_id_type=pl.DeviceIdType.MESH)

    def wkv_copies(t):
        res = []
        for i in range(2):
            col = pl.multiple_of((h * heads + 2 * t + i) * DH, DH)
            for j, w in enumerate((wk_hbm, wv_hbm)):
                dst = wkv.at[t, :, pl.ds((2 * i + j) * DH, DH)]
                res.append(pltpu.make_async_copy(w.at[:, pl.ds(col, DH)], dst, wkv_sem.at[t, i, j]))
        return res

    qt = wq.shape[-1]
    n_q = wq.shape[0]

    def wq_copy(t):
        col = pl.multiple_of(h * qcols + t * qt, qt)
        return pltpu.make_async_copy(wq_hbm.at[:, pl.ds(col, qt)], wq.at[t], wq_sem.at[t])

    def wo_copies(g):
        res = []
        for i, core in enumerate((h, other)):
            row = pl.multiple_of(core * qcols + g * gw, DH)
            res.append(pltpu.make_async_copy(wo_hbm.at[pl.ds(row, gw)], wo.at[g, pl.ds(i * gw, gw)], wo_sem.at[g, i]))
        return res

    def own(g, r, to_right):
        s = 0 if to_right else 1
        ref = kv.at[g, :, c, r]
        return remote(ref, ref, own_send.at[s, g, r], near_recv.at[s, g, r], right if to_right else left)

    def near_wait(g, r, from_left):
        s = 0 if from_left else 1
        ref = kv.at[g, :, left_chip if from_left else right_chip, r]
        remote(ref, ref, own_send.at[s, g, r], near_recv.at[s, g, r], right if from_left else left).wait_recv()

    def fwd(g, to_right):
        s = 0 if to_right else 1
        ref = kv.at[g, :, left_chip if to_right else right_chip, 0 if to_right else 1]
        return remote(ref, ref, fwd_send.at[s, g], far_recv.at[s, g], right if to_right else left)

    def far_wait(g):
        for s in range(2):
            ref = kv.at[g, :, far_chip, s]
            remote(ref, ref, fwd_send.at[s, g], far_recv.at[s, g], right if s == 0 else left).wait_recv()

    def forward(g):
        for to_right in (True, False):
            near_wait(g, 0 if to_right else 1, to_right)
            fwd(g, to_right).start()

    def send_rows(g, r):
        own(g, r, True).start()
        own(g, r, False).start()

    def send_first(g):
        own(g, 0, True).start()
        own(g, 1, False).start()

    def send_second(g):
        own(g, 1, True).start()
        own(g, 0, False).start()

    def proj_kv(t, r):
        src = x_buf[:, r].reshape(rows, dim)
        res = jnp.dot(src, wkv[t], preferred_element_type=F32)
        for i in range(2):
            kv[2 * t + i, :, c, r, 0] = res[:, 2 * i * DH:(2 * i + 1) * DH].astype(BF16).reshape(2, piece, DH)
            for f in range(2):
                v = res[f * piece:(f + 1) * piece, (2 * i + 1) * DH:2 * (i + 1) * DH]
                kv[2 * t + i, f, c, r, 1] = v.T.astype(BF16)

    def proj_q(t, r):
        src = x_buf[:, r].reshape(rows, dim)
        res = jnp.dot(src, wq[t], preferred_element_type=F32).astype(BF16)
        per = qt // DH
        for i in range(per):
            q_buf[per * t + i, :, r] = res[:, i * DH:(i + 1) * DH].reshape(2, piece, DH)

    def dyn(chip):
        return (chip > c).astype(jnp.int32)

    near_static = [(0, 0, c), (1, 1, c), (1, 0, c), (1, 0, left_chip), (1, 0, right_chip)]
    near_dyn = [(dyn(left_chip), dyn(left_chip), left_chip), (dyn(right_chip), dyn(right_chip), right_chip)]
    far_blocks = [(1, 0, far_chip), (dyn(far_chip), dyn(far_chip), far_chip)]
    blocks = near_static + near_dyn + far_blocks

    def first_row(half, dev):
        return jnp.where(half == 0, dev, 2 * n - 1 - dev) * piece

    def make_bias():
        for b, (qs, ks, kc) in enumerate(blocks):
            for r in range(2):
                dev = 2 * c + r
                sq = seg_all[dev, pl.ds(qs, 1)]
                pq = first_row(qs, dev) + lax.broadcasted_iota(jnp.int32, (piece, piece), 1)
                for kr in range(2):
                    kd = 2 * kc + kr
                    sk = jnp.broadcast_to(seg_all[kd, pl.ds(ks, 1)], (piece, piece)).T
                    pk = first_row(ks, kd) + lax.broadcasted_iota(jnp.int32, (piece, piece), 0)
                    ok = (sq == sk) & (pk <= pq)
                    bias[b, pl.ds(kr * piece, piece), pl.ds(r * piece, piece)] = jnp.where(ok, 0.0, NEG).astype(F32)

    def scores(g, j, b):
        qs, ks, kc = blocks[b]
        q = q_buf[g * groups + j, qs].reshape(rows, DH)
        k = kv[g, ks, kc, :, 0].reshape(rows, DH)
        s = lax.dot_general(k, q, (((1,), (1,)), ((), ())), preferred_element_type=F32)
        return s + bias[b]

    def top(s):
        return jnp.max(s, axis=0, keepdims=True)

    def values(g, b):
        return jnp.concatenate([kv[g, blocks[b][1], blocks[b][2], r, 1] for r in range(2)], axis=1)

    def region(fn):
        pl.when(me >= 0)(fn)

    def attend(g, bs, start):
        st = g % 2 * groups

        def score_all():
            for j in range(groups):
                m = [None, None] if start else [m_buf[st + j, 0], m_buf[st + j, 1]]
                for i, b in enumerate(bs):
                    s = scores(g, j, b)
                    s_buf[j, i] = s
                    t = top(s)
                    half = blocks[b][0]
                    for f in range(2):
                        if isinstance(half, int):
                            v = t if half == f else None
                        else:
                            v = jnp.where(half == f, t, NEG)
                        if v is not None:
                            m[f] = v if m[f] is None else jnp.maximum(m[f], v)
                for f in range(2):
                    if not start:
                        c_buf[j, f] = jnp.exp2(m_buf[st + j, f] * SCALE - m[f] * SCALE)
                    m_buf[st + j, f] = m[f]

        def weigh_all():
            for j in range(groups):
                l, a = [0.0, 0.0], [0.0, 0.0]
                if not start:
                    l = [l_buf[st + j, f] * c_buf[j, f] for f in range(2)]
                    a = [a_buf[st + j, f] * c_buf[j, f] for f in range(2)]
                late = []
                for i, b in enumerate(bs):
                    half = blocks[b][0]
                    p = jnp.exp2(s_buf[j, i] * SCALE - m_buf[st + j, half] * SCALE)
                    lb = jnp.sum(p, axis=0, keepdims=True)
                    ab = jnp.dot(values(g, b), p.astype(BF16), preferred_element_type=F32)
                    if isinstance(half, int):
                        l[half], a[half] = l[half] + lb, a[half] + ab
                    else:
                        late.append((half, lb, ab))
                if start:
                    for f in range(2):
                        l_buf[st + j, f], a_buf[st + j, f] = l[f], a[f]
                    for half, lb, ab in late:
                        l_buf[st + j, half] = l_buf[st + j, half] + lb
                        a_buf[st + j, half] = a_buf[st + j, half] + ab
                else:
                    for f in range(2):
                        for half, lb, ab in late:
                            l[f] = l[f] + jnp.where(half == f, lb, 0.0)
                            a[f] = a[f] + jnp.where(half == f, ab, 0.0)
                        o = a[f] * (1.0 / l[f])
                        o_buf[g, f, :, :, pl.ds(j * DH, DH)] = o.T.astype(BF16).reshape(2, piece, DH)

        region(score_all)
        region(weigh_all)

    near_ids = list(range(len(near_static) + len(near_dyn)))
    far_ids = [len(near_ids), len(near_ids) + 1]

    def near(g):
        attend(g, near_ids, True)

    def far(g):
        attend(g, far_ids, False)

    def o_send(g):
        return remote(o_buf.at[g, :, other], o_sib.at[g], os_send.at[g], os_recv.at[g], sibling)

    nt = 3
    tile = wo.shape[-1] // nt

    def mine(g):
        return o_buf[g, :, h].reshape(rows, gw)

    def theirs(g):
        return o_sib[g].reshape(rows, gw)

    def project(lhs, rhs, first, last):
        for t in range(nt):
            col = pl.ds(t * tile, tile)
            acc = jnp.dot(lhs, rhs(col), preferred_element_type=F32)
            if not first:
                acc = acc + y_acc[:, col]
            if last:
                y_out[:, col] = acc.astype(BF16)
            else:
                y_acc[:, col] = acc

    def wo_wait(g):
        for cp in wo_copies(g):
            cp.wait()

    def out_proj(gs):
        lhs = []
        for g in gs:
            wo_wait(g)
            o_send(g).wait_recv()
            lhs += [mine(g), theirs(g)]
        project(jnp.concatenate(lhs, axis=-1),
                lambda col: wo[pl.ds(gs[0], len(gs)), :, col].reshape(len(gs) * 2 * gw, tile), gs[0] == 0, False)

    x_own = pltpu.make_async_copy(x_hbm, x_buf.at[:, h], x_sem)
    x_own.start()
    seg_own = pltpu.make_async_copy(seg_hbm, seg_all.at[me], seg_sem)
    seg_own.start()
    n_kv = wkv.shape[0]
    barrier = pltpu.get_barrier_semaphore()
    for d in range(1, n):
        pl.semaphore_signal(barrier, inc=1, device_id={"cp": lax.rem(me + d, n)}, device_id_type=pl.DeviceIdType.MESH)
    for t in range(n_kv):
        for cp in wkv_copies(t):
            cp.start()
    for t in range(n_q):
        wq_copy(t).start(priority=1)

    with ph("wait_x"):
        x_own.wait()
        for cp in wkv_copies(0):
            cp.wait()
        seg_own.wait()
    with ph("kv0a"):
        proj_kv(0, h)

    with ph("barrier"):
        pl.semaphore_wait(barrier, n - 1)
    x_send = remote(x_buf.at[:, h], x_buf.at[:, h], xs_send, xs_recv, sibling)
    x_send.start()
    send_rows(0, h)
    send_rows(1, h)
    seg_sends = []
    for d in range(1, n):
        cp = remote(seg_all.at[me], seg_all.at[me], sg_send.at[d - 1], sg_recv.at[d - 1], lax.rem(me + d, n))
        cp.start()
        seg_sends.append(cp)
    for g in range(heads):
        for cp in wo_copies(g):
            cp.start(priority=1)
    with ph("kv1a"):
        for cp in wkv_copies(1):
            cp.wait()
        proj_kv(1, h)
    with ph("qa"):
        for t in range(n_q - 1):
            wq_copy(t).wait()
            proj_q(t, h)
    with ph("wait_xs"):
        remote(x_buf.at[:, other], x_buf.at[:, other], xs_send, xs_recv, sibling).wait_recv()
    with ph("kv0b"):
        proj_kv(0, other)
    send_rows(0, other)
    send_rows(1, other)
    with ph("kv1b"):
        proj_kv(1, other)
    with ph("qb"):
        wq_copy(n_q - 1).wait()
        proj_q(n_q - 1, h)
        for t in range(n_q):
            proj_q(t, other)
    with ph("wait_seg"):
        for d in range(1, n):
            src = lax.rem(me + n - d, n)
            remote(seg_all.at[src], seg_all.at[src], sg_send.at[d - 1], sg_recv.at[d - 1], src).wait_recv()
    with ph("bias"):
        make_bias()

    def near_rest(g):
        near_wait(g, 1, True)
        near_wait(g, 0, False)

    with ph("fwd0"):
        forward(0)
    send_first(2)
    send_second(2)
    with ph("nwait0"):
        near_rest(0)
    with ph("near0"):
        near(0)
    with ph("fwd1"):
        forward(1)
    send_first(3)
    send_second(3)
    with ph("nwait1"):
        near_rest(1)
    with ph("near1"):
        near(1)
    with ph("fwait0"):
        far_wait(0)
    with ph("far0"):
        far(0)
    o_send(0).start()
    with ph("fwd2"):
        forward(2)
    with ph("nwait2"):
        near_rest(2)
    with ph("near2"):
        near(2)
    with ph("fwait1"):
        far_wait(1)
    with ph("far1"):
        far(1)
    o_send(1).start()
    with ph("out0"):
        out_proj((0,))
    with ph("fwd3"):
        forward(3)
    with ph("out1"):
        out_proj((1,))
    with ph("nwait3"):
        near_rest(3)
    with ph("near3"):
        near(3)
    with ph("fwait2"):
        far_wait(2)
    with ph("far2"):
        far(2)
    o_send(2).start()
    with ph("fwait3"):
        far_wait(3)
    with ph("far3"):
        far(3)
    o_send(3).start()
    with ph("out2"):
        out_proj((2,))
    wo_wait(3)
    with ph("out3a"):
        project(mine(3), lambda col: wo[3, pl.ds(0, gw), col], False, False)
    with ph("owait"):
        o_send(3).wait_recv()
    with ph("out3b"):
        project(theirs(3), lambda col: wo[3, pl.ds(gw, gw), col], False, True)

    with ph("drain"):
        x_send.wait_send()
        for cp in seg_sends:
            cp.wait_send()
        for g in range(heads):
            for r in range(2):
                own(g, r, True).wait_send()
                own(g, r, False).wait_send()
            fwd(g, True).wait_send()
            fwd(g, False).wait_send()
            o_send(g).wait_send()


def solution(mesh):
    n = mesh.shape["cp"]
    chips = n // 2

    def local(x, seg, wq, wk, wv, wo):
        lq, d = x.shape
        piece = lq // 2
        kvh = wk.shape[1] // DH
        groups = wq.shape[1] // wk.shape[1]
        heads = kvh // 2
        qh = heads * groups
        dma = pltpu.SemaphoreType.DMA
        return pl.pallas_call(
            functools.partial(kernel, n, heads, groups),
            out_shape=pltpu.VMEM((lq, wo.shape[1]), BF16),
            in_specs=[pl.BlockSpec(memory_space=pl.ANY)] * 6,
            out_specs=pl.BlockSpec(memory_space=pltpu.VMEM),
            scratch_shapes=[
                pltpu.VMEM((2, 2, piece, d), BF16),
                pltpu.VMEM((heads // 2, d, 4 * DH), BF16),
                pltpu.VMEM((qh // 4, d, 4 * DH), BF16),
                pltpu.VMEM((heads, 2 * groups * DH, wo.shape[1]), BF16),
                pltpu.VMEM((heads, 2, chips, 2, 2, piece, DH), BF16),
                pltpu.VMEM((qh, 2, 2, piece, DH), BF16),
                pltpu.VMEM((n, 2, piece), jnp.int32),
                pltpu.VMEM((9, lq, lq), F32),
                pltpu.VMEM((groups, 7, lq, lq), F32),
                pltpu.VMEM((2 * groups, 2, 1, lq), F32),
                pltpu.VMEM((2 * groups, 2, 1, lq), F32),
                pltpu.VMEM((groups, 2, 1, lq), F32),
                pltpu.VMEM((2 * groups, 2, DH, lq), F32),
                pltpu.VMEM((heads, 2, 2, piece, groups * DH), BF16),
                pltpu.VMEM((heads, 2, piece, groups * DH), BF16),
                pltpu.VMEM((lq, wo.shape[1]), F32),
                dma, dma, dma, dma, dma((n - 1,)), dma((n - 1,)),
                dma((heads // 2, 2, 2)), dma((qh // 4,)), dma((heads, 2)),
                dma((2, heads, 2)), dma((2, heads, 2)), dma((2, heads)), dma((2, heads)),
                dma((heads,)), dma((heads,)),
            ],
            compiler_params=pltpu.CompilerParams(
                collective_id=0, has_side_effects=True, vmem_limit_bytes=67043328 - (2 << 20)),
            name="fused_attention",
        )(x.reshape(2, piece, d), seg.reshape(2, piece), wq, wk, wv, wo)

    rows = P(("dp", "cp"), None)
    return jax.shard_map(local, mesh=mesh, in_specs=(rows, P(("dp", "cp")), P(), P(), P(), P()), out_specs=rows, check_vma=False)
```

profile of v0, /device:TPU:113, one launch (start us, length us, event | category | flops | bytes accessed | tf_op | source)
XLA Modules:
  0.0 48.0 jit_solution(14362708727962964363)
XLA Ops:
  0.0 46.8 %fused_attention.1 = bf16[256,3072]{1,0:T(8,128)(2,1)S(1)} custom-call(bf16[2,128,3072]{2,1,0:T(8,128)(2,1)} %bitcast.2, s32[2,128]{1,0:T(2,128)} %bitcast.3, bf16[3072,3072]{1,0:T(8,128)(2,1)} %wq_hbm.1, bf16[3072,1024]{1,0:T(8,128)(2,1)} %wk_hbm.1, bf16[3072,1024]{1,0:T(8,128)(2,1)} %wv_hbm.1, bf16[3072,3072]{1,0:T(8,128)(2,1)} %wo_hbm.1), custom_call_target="tpu_custom_call" | custom-call | tf_op jit(solution)/shard_map/fused_attention/pallas_call | solution.py:416
  46.8 1.1 %copy.8 = bf16[256,3072]{1,0:T(8,128)(2,1)} copy(bf16[256,3072]{1,0:T(8,128)(2,1)S(1)} %fused_attention.1) | data formatting | bytes 3145728
where the time goes:
time: 48.4 us; the launch traced here: 48 us
  Pallas kernels  46.8 us (97%)
  local copies, waits for them, and re-layouts  1.15 us (2%)
    pallas_call x1, Pallas kernels, local(): pl.pallas_call(functools.partial(kernel, n, heads, groups), out_shape=plt...  46.8 us
    unnamed x1, local copies, waits for them, and re-layouts  1.15 us

commit v1 on v0

--- a/solution.py
+++ b/solution.py
@@ -20,9 +20,10 @@
     x_hbm, seg_hbm, wq_hbm, wk_hbm, wv_hbm, wo_hbm, y_out,
     x_buf, wkv, wq, wo, kv, q_buf, seg_all, bias, s_buf, m_buf, l_buf, c_buf, a_buf, o_buf, o_sib, y_acc,
     x_sem, xs_send, xs_recv, seg_sem, sg_send, sg_recv, wkv_sem, wq_sem, wo_sem,
-    own_send, near_recv, fwd_send, far_recv, os_send, os_recv,
+    kv_send, near_recv, far_recv, os_send, os_recv,
 ):
     chips = n // 2
+    parts = wkv_sem.shape[1]
     piece = x_hbm.shape[1]
     rows = 2 * piece
     dim = x_hbm.shape[2]
@@ -41,14 +42,20 @@
             src_ref=src, dst_ref=dst, send_sem=send, recv_sem=recv,
             device_id={"cp": dev}, device_id_type=pl.DeviceIdType.MESH)
 
-    def wkv_copies(t):
-        res = []
-        for i in range(2):
-            col = pl.multiple_of((h * heads + 2 * t + i) * DH, DH)
+    def wkv_part(g, part):
+        return (pl.ds(part * dim // parts, dim // parts), pl.ds(g % 2 * 2 * DH, 2 * DH))
+
+    def wkv_start(g):
+        col = pl.multiple_of((h * heads + g) * DH, DH)
+        for part in range(parts):
+            rng, at = wkv_part(g, part)
             for j, w in enumerate((wk_hbm, wv_hbm)):
-                dst = wkv.at[t, :, pl.ds((2 * i + j) * DH, DH)]
-                res.append(pltpu.make_async_copy(w.at[:, pl.ds(col, DH)], dst, wkv_sem.at[t, i, j]))
-        return res
+                dst = wkv.at[g // 2, rng, pl.ds(at.start + j * DH, DH)]
+                pltpu.make_async_copy(w.at[rng, pl.ds(col, DH)], dst, wkv_sem.at[g, part]).start()
+
+    def wkv_wait(g, part):
+        ref = wkv.at[g // 2, *wkv_part(g, part)]
+        pltpu.make_async_copy(ref, ref, wkv_sem.at[g, part]).wait()
 
     qt = wq.shape[-1]
     n_q = wq.shape[0]
@@ -61,28 +68,30 @@
         res = []
         for i, core in enumerate((h, other)):
             row = pl.multiple_of(core * qcols + g * gw, DH)
-            res.append(pltpu.make_async_copy(wo_hbm.at[pl.ds(row, gw)], wo.at[g, pl.ds(i * gw, gw)], wo_sem.at[g, i]))
+            res.append(pltpu.make_async_copy(wo_hbm.at[pl.ds(row, gw)], wo.at[g, pl.ds(i * gw, gw)], wo_sem.at[g]))
         return res
+
+    seg_others = seg_all.at[pl.ds(0, n - 1)]
 
     def own(g, r, to_right):
         s = 0 if to_right else 1
         ref = kv.at[g, :, c, r]
-        return remote(ref, ref, own_send.at[s, g, r], near_recv.at[s, g, r], right if to_right else left)
+        return remote(ref, ref, kv_send.at[g], near_recv.at[s, g, r], right if to_right else left)
 
     def near_wait(g, r, from_left):
         s = 0 if from_left else 1
         ref = kv.at[g, :, left_chip if from_left else right_chip, r]
-        remote(ref, ref, own_send.at[s, g, r], near_recv.at[s, g, r], right if from_left else left).wait_recv()
+        remote(ref, ref, kv_send.at[g], near_recv.at[s, g, r], right if from_left else left).wait_recv()
 
     def fwd(g, to_right):
         s = 0 if to_right else 1
         ref = kv.at[g, :, left_chip if to_right else right_chip, 0 if to_right else 1]
-        return remote(ref, ref, fwd_send.at[s, g], far_recv.at[s, g], right if to_right else left)
+        return remote(ref, ref, kv_send.at[g], far_recv.at[s, g], right if to_right else left)
 
     def far_wait(g):
         for s in range(2):
             ref = kv.at[g, :, far_chip, s]
-            remote(ref, ref, fwd_send.at[s, g], far_recv.at[s, g], right if s == 0 else left).wait_recv()
+            remote(ref, ref, kv_send.at[g], far_recv.at[s, g], right if s == 0 else left).wait_recv()
 
     def forward(g):
         for to_right in (True, False):
@@ -101,14 +110,26 @@
         own(g, 1, True).start()
         own(g, 0, False).start()
 
+    def keep_kv(g, r, k, v):
+        kv[g, :, c, r, 0] = k.astype(BF16).reshape(2, piece, DH)
+        for f in range(2):
+            kv[g, f, c, r, 1] = v[f * piece:(f + 1) * piece].T.astype(BF16)
+
+    def proj_head(g, r):
+        res = 0.0
+        for part in range(parts):
+            wkv_wait(g, part)
+            rng, at = wkv_part(g, part)
+            src = x_buf[:, r, :, rng].reshape(rows, rng.size)
+            res = res + jnp.dot(src, wkv[g // 2, rng, at], preferred_element_type=F32)
+        keep_kv(g, r, res[:, :DH], res[:, DH:])
+
     def proj_kv(t, r):
         src = x_buf[:, r].reshape(rows, dim)
         res = jnp.dot(src, wkv[t], preferred_element_type=F32)
         for i in range(2):
-            kv[2 * t + i, :, c, r, 0] = res[:, 2 * i * DH:(2 * i + 1) * DH].astype(BF16).reshape(2, piece, DH)
-            for f in range(2):
-                v = res[f * piece:(f + 1) * piece, (2 * i + 1) * DH:2 * (i + 1) * DH]
-                kv[2 * t + i, f, c, r, 1] = v.T.astype(BF16)
+            k = 2 * i * DH
+            keep_kv(2 * t + i, r, res[:, k:k + DH], res[:, k + DH:k + 2 * DH])
 
     def proj_q(t, r):
         src = x_buf[:, r].reshape(rows, dim)
@@ -157,12 +178,11 @@
     def region(fn):
         pl.when(me >= 0)(fn)
 
-    def attend(g, bs, start):
-        st = g % 2 * groups
-
+    def attend(g, bs, first, last):
         def score_all():
             for j in range(groups):
-                m = [None, None] if start else [m_buf[st + j, 0], m_buf[st + j, 1]]
+                k = g * groups + j
+                m = [None, None] if first else [m_buf[k, 0], m_buf[k, 1]]
                 for i, b in enumerate(bs):
                     s = scores(g, j, b)
                     s_buf[j, i] = s
@@ -176,54 +196,55 @@
                         if v is not None:
                             m[f] = v if m[f] is None else jnp.maximum(m[f], v)
                 for f in range(2):
-                    if not start:
-                        c_buf[j, f] = jnp.exp2(m_buf[st + j, f] * SCALE - m[f] * SCALE)
-                    m_buf[st + j, f] = m[f]
+                    if not first:
+                        c_buf[j, f] = jnp.exp2(m_buf[k, f] * SCALE - m[f] * SCALE)
+                    m_buf[k, f] = m[f]
 
         def weigh_all():
             for j in range(groups):
+                k = g * groups + j
                 l, a = [0.0, 0.0], [0.0, 0.0]
-                if not start:
-                    l = [l_buf[st + j, f] * c_buf[j, f] for f in range(2)]
-                    a = [a_buf[st + j, f] * c_buf[j, f] for f in range(2)]
+                if not first:
+                    l = [l_buf[k, f] * c_buf[j, f] for f in range(2)]
+                    a = [a_buf[k, f] * c_buf[j, f] for f in range(2)]
                 late = []
                 for i, b in enumerate(bs):
                     half = blocks[b][0]
-                    p = jnp.exp2(s_buf[j, i] * SCALE - m_buf[st + j, half] * SCALE)
+                    p = jnp.exp2(s_buf[j, i] * SCALE - m_buf[k, half] * SCALE)
                     lb = jnp.sum(p, axis=0, keepdims=True)
                     ab = jnp.dot(values(g, b), p.astype(BF16), preferred_element_type=F32)
                     if isinstance(half, int):
                         l[half], a[half] = l[half] + lb, a[half] + ab
                     else:
                         late.append((half, lb, ab))
-                if start:
-                    for f in range(2):
-                        l_buf[st + j, f], a_buf[st + j, f] = l[f], a[f]
-                    for half, lb, ab in late:
-                        l_buf[st + j, half] = l_buf[st + j, half] + lb
-                        a_buf[st + j, half] = a_buf[st + j, half] + ab
-                else:
+                if last:
                     for f in range(2):
                         for half, lb, ab in late:
                             l[f] = l[f] + jnp.where(half == f, lb, 0.0)
                             a[f] = a[f] + jnp.where(half == f, ab, 0.0)
                         o = a[f] * (1.0 / l[f])
                         o_buf[g, f, :, :, pl.ds(j * DH, DH)] = o.T.astype(BF16).reshape(2, piece, DH)
+                else:
+                    for f in range(2):
+                        l_buf[k, f], a_buf[k, f] = l[f], a[f]
+                    for half, lb, ab in late:
+                        l_buf[k, half] = l_buf[k, half] + lb
+                        a_buf[k, half] = a_buf[k, half] + ab
 
         region(score_all)
         region(weigh_all)
 
-    near_ids = list(range(len(near_static) + len(near_dyn)))
-    far_ids = [len(near_ids), len(near_ids) + 1]
+    def here(g):
+        attend(g, [0, 1, 2], True, False)
 
     def near(g):
-        attend(g, near_ids, True)
+        attend(g, [3, 4, 5, 6], False, False)
 
     def far(g):
-        attend(g, far_ids, False)
+        attend(g, [7, 8], False, True)
 
     def o_send(g):
-        return remote(o_buf.at[g, :, other], o_sib.at[g], os_send.at[g], os_recv.at[g], sibling)
+        return remote(o_buf.at[g, :, other], o_sib.at[g], os_send, os_recv.at[g], sibling)
 
     nt = 3
     tile = wo.shape[-1] // nt
@@ -246,8 +267,7 @@
                 y_acc[:, col] = acc
 
     def wo_wait(g):
-        for cp in wo_copies(g):
-            cp.wait()
+        pltpu.make_async_copy(wo.at[g], wo.at[g], wo_sem.at[g]).wait()
 
     def out_proj(gs):
         lhs = []
@@ -262,41 +282,37 @@
     x_own.start()
     seg_own = pltpu.make_async_copy(seg_hbm, seg_all.at[me], seg_sem)
     seg_own.start()
-    n_kv = wkv.shape[0]
     barrier = pltpu.get_barrier_semaphore()
     for d in range(1, n):
         pl.semaphore_signal(barrier, inc=1, device_id={"cp": lax.rem(me + d, n)}, device_id_type=pl.DeviceIdType.MESH)
-    for t in range(n_kv):
-        for cp in wkv_copies(t):
-            cp.start()
+    for g in range(heads):
+        wkv_start(g)
     for t in range(n_q):
         wq_copy(t).start(priority=1)
 
     with ph("wait_x"):
         x_own.wait()
-        for cp in wkv_copies(0):
-            cp.wait()
         seg_own.wait()
     with ph("kv0a"):
-        proj_kv(0, h)
+        proj_head(0, h)
 
     with ph("barrier"):
         pl.semaphore_wait(barrier, n - 1)
     x_send = remote(x_buf.at[:, h], x_buf.at[:, h], xs_send, xs_recv, sibling)
     x_send.start()
     send_rows(0, h)
-    send_rows(1, h)
-    seg_sends = []
     for d in range(1, n):
-        cp = remote(seg_all.at[me], seg_all.at[me], sg_send.at[d - 1], sg_recv.at[d - 1], lax.rem(me + d, n))
-        cp.start()
-        seg_sends.append(cp)
+        remote(seg_all.at[me], seg_all.at[me], sg_send, sg_recv, lax.rem(me + d, n)).start()
     for g in range(heads):
         for cp in wo_copies(g):
             cp.start(priority=1)
+    with ph("kv0c"):
+        proj_head(1, h)
+    send_rows(1, h)
     with ph("kv1a"):
-        for cp in wkv_copies(1):
-            cp.wait()
+        for g in range(2, heads):
+            for part in range(parts):
+                wkv_wait(g, part)
         proj_kv(1, h)
     with ph("qa"):
         for t in range(n_q - 1):
@@ -316,9 +332,7 @@
         for t in range(n_q):
             proj_q(t, other)
     with ph("wait_seg"):
-        for d in range(1, n):
-            src = lax.rem(me + n - d, n)
-            remote(seg_all.at[src], seg_all.at[src], sg_send.at[d - 1], sg_recv.at[d - 1], src).wait_recv()
+        remote(seg_others, seg_others, sg_send, sg_recv, sibling).wait_recv()
     with ph("bias"):
         make_bias()
 
@@ -330,6 +344,8 @@
         forward(0)
     send_first(2)
     send_second(2)
+    with ph("here0"):
+        here(0)
     with ph("nwait0"):
         near_rest(0)
     with ph("near0"):
@@ -337,7 +353,8 @@
     with ph("fwd1"):
         forward(1)
     send_first(3)
-    send_second(3)
+    with ph("here1"):
+        here(1)
     with ph("nwait1"):
         near_rest(1)
     with ph("near1"):
@@ -347,8 +364,13 @@
     with ph("far0"):
         far(0)
     o_send(0).start()
+    with ph("here2"):
+        here(2)
     with ph("fwd2"):
         forward(2)
+    send_second(3)
+    with ph("here3"):
+        here(3)
     with ph("nwait2"):
         near_rest(2)
     with ph("near2"):
@@ -364,22 +386,22 @@
         forward(3)
     with ph("out1"):
         out_proj((1,))
-    with ph("nwait3"):
-        near_rest(3)
-    with ph("near3"):
-        near(3)
     with ph("fwait2"):
         far_wait(2)
     with ph("far2"):
         far(2)
     o_send(2).start()
+    with ph("nwait3"):
+        near_rest(3)
+    with ph("near3"):
+        near(3)
+    with ph("out2"):
+        out_proj((2,))
     with ph("fwait3"):
         far_wait(3)
     with ph("far3"):
         far(3)
     o_send(3).start()
-    with ph("out2"):
-        out_proj((2,))
     wo_wait(3)
     with ph("out3a"):
         project(mine(3), lambda col: wo[3, pl.ds(0, gw), col], False, False)
@@ -390,15 +412,11 @@
 
     with ph("drain"):
         x_send.wait_send()
-        for cp in seg_sends:
-            cp.wait_send()
+        remote(seg_others, seg_others, sg_send, sg_recv, sibling).wait_send()
         for g in range(heads):
-            for r in range(2):
-                own(g, r, True).wait_send()
-                own(g, r, False).wait_send()
-            fwd(g, True).wait_send()
-            fwd(g, False).wait_send()
-            o_send(g).wait_send()
+            sent = kv.at[g, :, pl.ds(0, chips - 1)]
+            remote(sent, sent, kv_send.at[g], near_recv.at[0, 0, 0], right).wait_send()
+        remote(o_sib, o_sib, os_send, os_recv.at[0], sibling).wait_send()
 
 
 def solution(mesh):
@@ -427,18 +445,18 @@
                 pltpu.VMEM((qh, 2, 2, piece, DH), BF16),
                 pltpu.VMEM((n, 2, piece), jnp.int32),
                 pltpu.VMEM((9, lq, lq), F32),
-                pltpu.VMEM((groups, 7, lq, lq), F32),
-                pltpu.VMEM((2 * groups, 2, 1, lq), F32),
-                pltpu.VMEM((2 * groups, 2, 1, lq), F32),
+                pltpu.VMEM((groups, 4, lq, lq), F32),
+                pltpu.VMEM((qh, 2, 1, lq), F32),
+                pltpu.VMEM((qh, 2, 1, lq), F32),
                 pltpu.VMEM((groups, 2, 1, lq), F32),
-                pltpu.VMEM((2 * groups, 2, DH, lq), F32),
+                pltpu.VMEM((qh, 2, DH, lq), F32),
                 pltpu.VMEM((heads, 2, 2, piece, groups * DH), BF16),
                 pltpu.VMEM((heads, 2, piece, groups * DH), BF16),
                 pltpu.VMEM((lq, wo.shape[1]), F32),
-                dma, dma, dma, dma, dma((n - 1,)), dma((n - 1,)),
-                dma((heads // 2, 2, 2)), dma((qh // 4,)), dma((heads, 2)),
-                dma((2, heads, 2)), dma((2, heads, 2)), dma((2, heads)), dma((2, heads)),
-                dma((heads,)), dma((heads,)),
+                dma, dma, dma, dma, dma, dma,
+                dma((heads, 4)), dma((qh // 4,)), dma((heads,)),
+                dma((heads,)), dma((2, heads, 2)), dma((2, heads)),
+                dma, dma((heads,)),
             ],
             compiler_params=pltpu.CompilerParams(
                 collective_id=0, has_side_effects=True, vmem_limit_bytes=67043328 - (2 << 20)),

time: 48.4 us -> 47.1 us (0.973)
  Pallas kernels: 46.8 us -> 45.9 us
    pallas_call x1, Pallas kernels: 46.8 us -> 45.9 us  [local(): pl.pallas_call(functools.partial(kernel, n, heads, groups), out_shape=plt...]
where the time goes in v1:
time: 47.1 us; the launch traced here: 47 us
  Pallas kernels  45.9 us (97%)
  local copies, waits for them, and re-layouts  1.15 us (2%)
    pallas_call x1, Pallas kernels, local(): pl.pallas_call(functools.partial(kernel, n, heads, groups), out_shape=plt...  45.9 us
    unnamed x1, local copies, waits for them, and re-layouts  1.15 us

profile of v1, /device:TPU:113, one launch (start us, length us, event | category | flops | bytes accessed | tf_op | source)
XLA Modules:
  0.0 47.0 jit_solution(1525402778230654439)
XLA Ops:
  0.0 45.9 %fused_attention.1 = bf16[256,3072]{1,0:T(8,128)(2,1)S(1)} custom-call(bf16[2,128,3072]{2,1,0:T(8,128)(2,1)} %bitcast.2, s32[2,128]{1,0:T(2,128)} %bitcast.3, bf16[3072,3072]{1,0:T(8,128)(2,1)} %wq_hbm.1, bf16[3072,1024]{1,0:T(8,128)(2,1)} %wk_hbm.1, bf16[3072,1024]{1,0:T(8,128)(2,1)} %wv_hbm.1, bf16[3072,3072]{1,0:T(8,128)(2,1)} %wo_hbm.1), custom_call_target="tpu_custom_call" | custom-call | tf_op jit(solution)/shard_map/fused_attention/pallas_call | solution.py:434
  45.9 1.1 %copy.8 = bf16[256,3072]{1,0:T(8,128)(2,1)} copy(bf16[256,3072]{1,0:T(8,128)(2,1)S(1)} %fused_attention.1) | data formatting | bytes 3145728

commit v2 on v1

--- a/solution.py
+++ b/solution.py
@@ -83,20 +83,25 @@
         ref = kv.at[g, :, left_chip if from_left else right_chip, r]
         remote(ref, ref, kv_send.at[g], near_recv.at[s, g, r], right if from_left else left).wait_recv()
 
+    def halves(g):
+        return ((g, slice(None)),) if g < heads - 1 else ((g, pl.ds(0, 1)), (heads, pl.ds(1, 1)))
+
     def fwd(g, to_right):
         s = 0 if to_right else 1
-        ref = kv.at[g, :, left_chip if to_right else right_chip, 0 if to_right else 1]
-        return remote(ref, ref, kv_send.at[g], far_recv.at[s, g], right if to_right else left)
-
-    def far_wait(g):
+        refs = [(i, kv.at[g, f, left_chip if to_right else right_chip, s]) for i, f in halves(g)]
+        return [remote(ref, ref, kv_send.at[g], far_recv.at[s, i], right if to_right else left) for i, ref in refs]
+
+    def far_wait(g, half=0):
+        i, f = halves(g)[half]
         for s in range(2):
-            ref = kv.at[g, :, far_chip, s]
-            remote(ref, ref, kv_send.at[g], far_recv.at[s, g], right if s == 0 else left).wait_recv()
+            ref = kv.at[g, f, far_chip, s]
+            remote(ref, ref, kv_send.at[g], far_recv.at[s, i], right if s == 0 else left).wait_recv()
 
     def forward(g):
         for to_right in (True, False):
             near_wait(g, 0 if to_right else 1, to_right)
-            fwd(g, to_right).start()
+            for cp in fwd(g, to_right):
+                cp.start()
 
     def send_rows(g, r):
         own(g, r, True).start()
@@ -293,13 +298,13 @@
     with ph("wait_x"):
         x_own.wait()
         seg_own.wait()
-    with ph("kv0a"):
-        proj_head(0, h)
 
     with ph("barrier"):
         pl.semaphore_wait(barrier, n - 1)
     x_send = remote(x_buf.at[:, h], x_buf.at[:, h], xs_send, xs_recv, sibling)
     x_send.start()
+    with ph("kv0a"):
+        proj_head(0, h)
     send_rows(0, h)
     for d in range(1, n):
         remote(seg_all.at[me], seg_all.at[me], sg_send, sg_recv, lax.rem(me + d, n)).start()
@@ -391,16 +396,22 @@
     with ph("far2"):
         far(2)
     o_send(2).start()
+    with ph("out2"):
+        pl.when(h == 0)(lambda: out_proj((2,)))
     with ph("nwait3"):
         near_rest(3)
     with ph("near3"):
         near(3)
-    with ph("out2"):
-        out_proj((2,))
+    with ph("out2b"):
+        pl.when(h == 1)(lambda: out_proj((2,)))
     with ph("fwait3"):
         far_wait(3)
     with ph("far3"):
-        far(3)
+        attend(3, [7], False, False)
+    with ph("fwait3b"):
+        far_wait(3, 1)
+    with ph("far3b"):
+        attend(3, [8], False, True)
     o_send(3).start()
     wo_wait(3)
     with ph("out3a"):
@@ -455,7 +466,7 @@
                 pltpu.VMEM((lq, wo.shape[1]), F32),
                 dma, dma, dma, dma, dma, dma,
                 dma((heads, 4)), dma((qh // 4,)), dma((heads,)),
-                dma((heads,)), dma((2, heads, 2)), dma((2, heads)),
+                dma((heads,)), dma((2, heads, 2)), dma((2, heads + 1)),
                 dma, dma((heads,)),
             ],
             compiler_params=pltpu.CompilerParams(

time: 47.1 us -> 46.3 us (0.983)
  Pallas kernels: 45.9 us -> 45 us
    pallas_call x1, Pallas kernels: 45.9 us -> 45 us  [local(): pl.pallas_call(functools.partial(kernel, n, heads, groups), out_shape=plt...]
where the time goes in v2:
time: 46.3 us; the launch traced here: 46.2 us
  Pallas kernels  45 us (97%)
  local copies, waits for them, and re-layouts  1.15 us (2%)
    pallas_call x1, Pallas kernels, local(): pl.pallas_call(functools.partial(kernel, n, heads, groups), out_shape=plt...  45 us
    unnamed x1, local copies, waits for them, and re-layouts  1.15 us

profile of v2, /device:TPU:113, one launch (start us, length us, event | category | flops | bytes accessed | tf_op | source)
XLA Modules:
  0.0 46.2 jit_solution(14048985755235112258)
XLA Ops:
  0.0 45.0 %fused_attention.1 = bf16[256,3072]{1,0:T(8,128)(2,1)S(1)} custom-call(bf16[2,128,3072]{2,1,0:T(8,128)(2,1)} %bitcast.2, s32[2,128]{1,0:T(2,128)} %bitcast.3, bf16[3072,3072]{1,0:T(8,128)(2,1)} %wq_hbm.1, bf16[3072,1024]{1,0:T(8,128)(2,1)} %wk_hbm.1, bf16[3072,1024]{1,0:T(8,128)(2,1)} %wv_hbm.1, bf16[3072,3072]{1,0:T(8,128)(2,1)} %wo_hbm.1), custom_call_target="tpu_custom_call" | custom-call | tf_op jit(solution)/shard_map/fused_attention/pallas_call | solution.py:445
  45.0 1.1 %copy.8 = bf16[256,3072]{1,0:T(8,128)(2,1)} copy(bf16[256,3072]{1,0:T(8,128)(2,1)S(1)} %fused_attention.1) | data formatting | bytes 3145728

commit v3 on v2

--- a/solution.py
+++ b/solution.py
@@ -45,17 +45,20 @@
     def wkv_part(g, part):
         return (pl.ds(part * dim // parts, dim // parts), pl.ds(g % 2 * 2 * DH, 2 * DH))
 
+    def wkv_at(g, part):
+        return wkv_sem.at[g, part] if g < 2 else wkv_sem.at[2, 0]
+
     def wkv_start(g):
         col = pl.multiple_of((h * heads + g) * DH, DH)
         for part in range(parts):
             rng, at = wkv_part(g, part)
             for j, w in enumerate((wk_hbm, wv_hbm)):
                 dst = wkv.at[g // 2, rng, pl.ds(at.start + j * DH, DH)]
-                pltpu.make_async_copy(w.at[rng, pl.ds(col, DH)], dst, wkv_sem.at[g, part]).start()
+                pltpu.make_async_copy(w.at[rng, pl.ds(col, DH)], dst, wkv_at(g, part)).start()
 
     def wkv_wait(g, part):
         ref = wkv.at[g // 2, *wkv_part(g, part)]
-        pltpu.make_async_copy(ref, ref, wkv_sem.at[g, part]).wait()
+        pltpu.make_async_copy(ref, ref, wkv_at(g, part)).wait()
 
     qt = wq.shape[-1]
     n_q = wq.shape[0]
@@ -251,6 +254,10 @@
     def o_send(g):
         return remote(o_buf.at[g, :, other], o_sib.at[g], os_send, os_recv.at[g], sibling)
 
+    def o_start(g):
+        for f in range(2):
+            remote(o_buf.at[g, f, other], o_sib.at[g, f], os_send, os_recv.at[g], sibling).start()
+
     nt = 3
     tile = wo.shape[-1] // nt
 
@@ -315,9 +322,7 @@
         proj_head(1, h)
     send_rows(1, h)
     with ph("kv1a"):
-        for g in range(2, heads):
-            for part in range(parts):
-                wkv_wait(g, part)
+        pltpu.make_async_copy(wkv.at[1], wkv.at[1], wkv_at(2, 0)).wait()
         proj_kv(1, h)
     with ph("qa"):
         for t in range(n_q - 1):
@@ -368,7 +373,7 @@
         far_wait(0)
     with ph("far0"):
         far(0)
-    o_send(0).start()
+    o_start(0)
     with ph("here2"):
         here(2)
     with ph("fwd2"):
@@ -384,7 +389,7 @@
         far_wait(1)
     with ph("far1"):
         far(1)
-    o_send(1).start()
+    o_start(1)
     with ph("out0"):
         out_proj((0,))
     with ph("fwd3"):
@@ -395,7 +400,7 @@
         far_wait(2)
     with ph("far2"):
         far(2)
-    o_send(2).start()
+    o_start(2)
     with ph("out2"):
         pl.when(h == 0)(lambda: out_proj((2,)))
     with ph("nwait3"):
@@ -412,7 +417,7 @@
         far_wait(3, 1)
     with ph("far3b"):
         attend(3, [8], False, True)
-    o_send(3).start()
+    o_start(3)
     wo_wait(3)
     with ph("out3a"):
         project(mine(3), lambda col: wo[3, pl.ds(0, gw), col], False, False)
@@ -465,7 +470,7 @@
                 pltpu.VMEM((heads, 2, piece, groups * DH), BF16),
                 pltpu.VMEM((lq, wo.shape[1]), F32),
                 dma, dma, dma, dma, dma, dma,
-                dma((heads, 4)), dma((qh // 4,)), dma((heads,)),
+                dma((3, 4)), dma((qh // 4,)), dma((heads,)),
                 dma((heads,)), dma((2, heads, 2)), dma((2, heads + 1)),
                 dma, dma((heads,)),
             ],

time: 46.3 us -> 46.2 us (level)
  no operation moved by 1% of the time
where the time goes in v3:
time: 46.2 us
  Pallas kernels  45 us (97%)
  local copies, waits for them, and re-layouts  1.15 us (2%)
    pallas_call x1, Pallas kernels, local(): pl.pallas_call(functools.partial(kernel, n, heads, groups), out_shape=plt...  45 us
    unnamed x1, local copies, waits for them, and re-layouts  1.15 us

profile of v3, /device:TPU:113, one launch (start us, length us, event | category | flops | bytes accessed | tf_op | source)
XLA Modules:
  0.0 46.2 jit_solution(12608878912312220350)
XLA Ops:
  0.0 45.0 %fused_attention.1 = bf16[256,3072]{1,0:T(8,128)(2,1)S(1)} custom-call(bf16[2,128,3072]{2,1,0:T(8,128)(2,1)} %bitcast.2, s32[2,128]{1,0:T(2,128)} %bitcast.3, bf16[3072,3072]{1,0:T(8,128)(2,1)} %wq_hbm.1, bf16[3072,1024]{1,0:T(8,128)(2,1)} %wk_hbm.1, bf16[3072,1024]{1,0:T(8,128)(2,1)} %wv_hbm.1, bf16[3072,3072]{1,0:T(8,128)(2,1)} %wo_hbm.1), custom_call_target="tpu_custom_call" | custom-call | tf_op jit(solution)/shard_map/fused_attention/pallas_call | solution.py:450
  45.0 1.1 %copy.8 = bf16[256,3072]{1,0:T(8,128)(2,1)} copy(bf16[256,3072]{1,0:T(8,128)(2,1)S(1)} %fused_attention.1) | data formatting | bytes 3145728
